TPU v7x, 32 devices: a whole 2x2x4 slice. The times are simulated.
32 devices in a mesh: group: 4 (over x, core), bl: 8 (over z, y).
Axes of the slice: x: 2, y: 2, z: 4, core: 2. Of those that a mesh axis runs over, the one named last changes fastest.
Arguments:
- visibilities: float32 [2, 512, 16, 1024], P(None, ('group', 'bl')), parts along dimension 1, may hold values from -400 to 400
- flags: int32 [512, 8], P(('group', 'bl')), parts along dimension 0, may hold values 0 or 1
Outputs:
- cross_power: float32 [32, 512, 128], P(None, ('group', 'bl')), parts along dimension 1
- bandpower: float32 [128], P('group'), parts along dimension 0
There are 4 independent parts, one for each index of `group`. A program takes and returns all parts, laid end to end along the dimension named above; each array names one. Nothing has to cross between parts.
All inputs are finite; a program needn't handle non-finite values. No bound on the sum of `flags` on one device may be relied on, other than what follows from the above.
Results may differ from a plain program's by a relative error of at most 0.004.
Values may be sent and summed in bfloat16 or wider, within the bound.
A program may use at most 192 MiB of HBM per device.

v0:
```python
import math

import jax
import jax.numpy as jnp
from jax import lax
from jax.sharding import PartitionSpec as P

NF = 1024
NT = 16
CB = 128
BW = 32


def make_taper():
    angle = jnp.arange(NF, dtype=jnp.int32).astype(jnp.float32) * (2.0 * math.pi / (NF - 1))
    return (
        0.35875
        - 0.48829 * jnp.cos(angle)
        + 0.14128 * jnp.cos(2.0 * angle)
        - 0.01168 * jnp.cos(3.0 * angle)
    )


def make_tables():
    index = jnp.arange(NF, dtype=jnp.int32)
    phase = index[:, None] * index[None, :] % NF
    angle = phase.astype(jnp.float32) * (2.0 * math.pi / NF)
    return (jnp.cos(angle), jnp.sin(angle))


def delay_spectra(visibilities, flags):
    count = visibilities.shape[1]
    keep = (
        jnp.broadcast_to(flags[:, :, None], (count, NF // CB, CB))
        .reshape(count, NF)
        .astype(jnp.float32)
    )
    weight = keep * make_taper()[None, :]
    tapered = visibilities * weight[None, :, None, :]
    real_rows = tapered[0].reshape(count * NT, NF)
    imag_rows = tapered[1].reshape(count * NT, NF)
    cosine, sine = make_tables()
    high = lax.Precision.HIGHEST
    scale = 1.0 / math.sqrt(NF)
    real_out = (
        jnp.dot(real_rows, cosine, precision=high) + jnp.dot(imag_rows, sine, precision=high)
    ) * scale
    imag_out = (
        jnp.dot(imag_rows, cosine, precision=high) - jnp.dot(real_rows, sine, precision=high)
    ) * scale
    stacked = jnp.stack([real_out.reshape(count, NT, NF), imag_out.reshape(count, NT, NF)], 2)
    stacked = stacked.reshape(count, NT, 2, NF // BW, BW).transpose(3, 0, 1, 2, 4)
    return stacked.reshape(NF // BW, count, NT * 2 * BW).astype(jnp.bfloat16)


def shards(visibilities, flags):
    own = delay_spectra(visibilities, flags)
    bands, rows, inner = own.shape
    total = rows * lax.axis_size("bl")
    whole = lax.all_gather(own, "bl", axis=1, tiled=True)
    cross_power = jnp.einsum("kbj,kcj->kbc", own, whole, preferred_element_type=jnp.float32) / NT
    own_wide = own.astype(jnp.float32)
    self_power = jnp.sum(own_wide * own_wide, axis=2) / NT
    partial_sum = jnp.sum(cross_power, axis=(1, 2)) - jnp.sum(self_power, axis=1)
    bandpower = lax.psum(partial_sum, "bl") / total
    return (cross_power, bandpower)


def solution(mesh):
    return jax.shard_map(
        shards,
        mesh=mesh,
        in_specs=(P(None, ("group", "bl"), None, None), P(("group", "bl"), None)),
        out_specs=(P(None, ("group", "bl"), None), P("group")),
        check_vma=False,
    )
```

profile of v0, /device:TPU:0, one launch (start us, length us, event | category | flops | bytes accessed | tf_op | source)
XLA Modules:
  0.0 277.9 jit_solution(7945520708464780710)
XLA Ops:
  7.2 0.0 all-gather.2.cloned.1.call-start
  7.2 0.1 multiply_subtract_fusion
  7.3 0.7 convert_element_type.43
  8.0 0.1 copy.6
  8.0 0.1 broadcast_in_dim.2
  8.1 1.8 broadcast_multiply_fusion
  10.0 0.2 fusion.45
  10.2 20.0 %fusion.8 = f32[256,1024]{1,0:T(8,128)S(1)} fusion(f32[256,1024]{1,0:T(8,128)S(1)} %bitcast.13), kind=kOutput, calls=%fused_computation.13 | convolution fusion | flops 3235905536 | bytes 2097152 | tf_op jit(solution)/shard_map/dot_general | solution.py:49
  30.2 20.0 %fusion.10 = f32[256,1024]{1,0:T(8,128)S(1)} fusion(f32[256,1024]{1,0:T(8,128)S(1)} %bitcast.15), kind=kOutput, calls=%fused_computation.14 | convolution fusion | flops 3235905536 | bytes 2097152 | tf_op jit(solution)/shard_map/dot_general | solution.py:46
  50.2 19.7 %fusion.22 = bf16[256,1024]{1,0:T(8,128)(2,1)S(1)} fusion(f32[256,1024]{1,0:T(8,128)S(1)} %fusion.8, f32[256,1024]{1,0:T(8,128)S(1)} %bitcast.16), kind=kOutput, calls=%fused_computation.19 | convolution fusion | flops 3236691968 | bytes 2621440 | tf_op jit(solution)/shard_map/dot_general | solution.py:49
  70.0 19.5 %fusion.25 = bf16[256,1024]{1,0:T(8,128)(2,1)S(1)} fusion(f32[256,1024]{1,0:T(8,128)S(1)} %fusion.10, f32[256,1024]{1,0:T(8,128)S(1)} %bitcast.14), kind=kOutput, calls=%fused_computation.20 | convolution fusion | flops 3236691968 | bytes 2621440 | tf_op jit(solution)/shard_map/dot_general | solution.py:46
  89.5 1.6 stack.7
  91.1 2.6 stack.8
  93.7 4.5 %fusion.28 = bf16[32,16,16,2,32]{4,0,2,1,3:T(8,128)(2,1)} fusion(bf16[16,16,1,32,32]{4,3,1,0,2:T(8,128)(2,1)} %stack.8, bf16[16,16,1,32,32]{4,3,1,0,2:T(8,128)(2,1)S(1)} %stack.7), kind=kLoop, calls=%fused_computation.23 | loop fusion | flops 524288 | bytes 2097152 | tf_op jit(solution)/shard_map/convert_element_type | solution.py:53
  98.2 8.4 %copy.7 = bf16[32,16,16,2,32]{4,3,2,1,0:T(2,128)(2,1)} copy(bf16[32,16,16,2,32]{4,0,2,1,3:T(8,128)(2,1)} %fusion.28) | data formatting | bytes 2097152 | tf_op jit(solution)/shard_map/convert_element_type | solution.py:53
  106.6 11.7 %convert_element_type.49 = bf16[32,16,1024]{2,1,0:T(8,128)(2,1)} reshape(bf16[32,16,16,2,32]{4,3,2,1,0:T(2,128)(2,1)} %copy.7) | data formatting | bytes 2097152 | tf_op jit(solution)/shard_map/convert_element_type | solution.py:53
  118.3 0.0 copy-start
  118.3 0.0 all-gather.2.cloned.1.call-update
  118.4 2.8 %multiply_reduce_fusion = f32[16,32]{1,0:T(8,128)S(1)} fusion(bf16[16,16,1,32,32]{4,3,1,0,2:T(8,128)(2,1)} %stack.8, bf16[16,16,1,32,32]{4,3,1,0,2:T(8,128)(2,1)S(1)} %stack.7), kind=kLoop, calls=%fused_computation.1 | loop fusion | flops 2096640 | bytes 1050624 | tf_op jit(solution)/shard_map/reduce_sum | solution.py:63
  121.2 124.5 %all-gather.2.cloned.1.call-done = bf16[32,128,1024]{2,1,0:T(8,128)(2,1)} async-done(((bf16[32,16,1024]{2,1,0:T(8,128)(2,1)}), bf16[32,128,1024]{2,1,0:T(8,128)(2,1)}) %all-gather.2.cloned.1.call-update) | async-done | bytes 8388624 | tf_op jit(solution)/shard_map/all_gather | solution.py:60
  245.7 0.0 copy-done
  245.7 6.4 %fusion.46 = (f32[32]{0:T(128)S(1)}, f32[32,16,128]{2,1,0:T(8,128)}) fusion(bf16[32,16,1024]{2,1,0:T(8,128)(2,1)S(1)} %copy-done, bf16[32,128,1024]{2,1,0:T(8,128)(2,1)} %all-gather.2.cloned.1.call-done), kind=kOutput, calls=%fused_computation.45 | convolution fusion | flops 134348768 | bytes 9699456 | tf_op jit(solution)/shard_map/kbj,kcj->kbc/dot_general | solution.py:61
  252.1 18.5 %psum.7 = f32[32]{0:T(128)S(1)} all-reduce(f32[32]{0:T(128)S(1)} %sub.27), channel_id=1, replica_groups=mesh['group'=4,'bl'=8] {'bl'}, use_global_device_ids=true, to_apply=%region_3.4 | all-reduce | flops 32 | bytes 256 | tf_op jit(solution)/shard_map/psum | solution.py:65
  270.6 0.5 broadcast_multiply_fusion.1
  (3 shorter events, 0.1 us)
Async XLA Ops:
  7.2 238.5 %all-gather.2.cloned.1.call-start = ((), (), s32[]{:S(2)}) async-start(), calls=%async_computation | async-start | bytes 9437184 | tf_op jit(solution)/shard_map/all_gather | solution.py:60
  118.3 127.4 %copy-start = (bf16[32,16,1024]{2,1,0:T(8,128)(2,1)S(1)}, bf16[32,16,1024]{2,1,0:T(8,128)(2,1)}, u32[]{:S(2)}) copy-start(bf16[32,16,1024]{2,1,0:T(8,128)(2,1)} %convert_element_type.49) | copy-start | bytes 3145732
Sparse Core Ops, SparseCore 0:
  118.5 127.1 all-gather.1
where the time goes:
time: 278 us
  waiting for transfers between devices  124 us (45%)
  matrix products  85.7 us (31%)
  local copies, waits for them, and re-layouts  24.7 us (9%)
  blocking collectives  18.5 us (7%)
  between operations  14.1 us (5%)
  other arithmetic  10.5 us (4%)
    all_gather x1, waiting for transfers between devices, shards(): whole = lax.all_gather(own, 'bl', axis=1, tiled=True)  124 us
    convert_element_type x2, local copies, waits for them, and re-layouts, delay_spectra(): return stacked.reshape(NF // BW, count, NT * 2 * BW).astype(jnp.bfloat16)  20.2 us
    dot_general x1, matrix products, delay_spectra(): jnp.dot(imag_rows, cosine, precision=high)  20 us
    dot_general x1, matrix products, delay_spectra(): jnp.dot(real_rows, cosine, precision=high)  20 us
    dot_general x1, matrix products, delay_spectra(): jnp.dot(real_rows, sine, precision=high)  19.7 us
    dot_general x1, matrix products, delay_spectra(): jnp.dot(imag_rows, sine, precision=high)  19.5 us
    psum x1, blocking collectives, shards(): bandpower = lax.psum(partial_sum, 'bl') / total  18.5 us
    dot_general x1, matrix products, shards(): jnp.einsum('kbj,kcj->kbc', own, whole, preferred_element_type=jnp.float32)  6.38 us
  transfers between devices with their start and end apart: 1, of which 1 were waited for; matrix products, arithmetic and copies ran while one was open for 1% of the time, Pallas kernels for 0%

commit v1 on v0

v1 whole, which is shorter than its diff:
```python
import functools
import math

import jax
import jax.numpy as jnp
import numpy as np
from jax import lax
from jax.experimental import pallas as pl
from jax.experimental.pallas import tpu as pltpu
from jax.sharding import PartitionSpec as P

BW = 32
LANES = 128
CHUNKS = 4
MESH = pl.DeviceIdType.MESH
F32 = jnp.float32
BF16 = jnp.bfloat16


def tables(nf, nt):
    radix = nf // LANES
    a = 2.0 * np.pi / (nf - 1) * np.arange(nf)
    taper = 0.35875 - 0.48829 * np.cos(a) + 0.14128 * np.cos(2 * a) - 0.01168 * np.cos(3 * a)
    n = np.arange(LANES)
    angle = 2.0 * np.pi * np.outer(np.arange(radix), n) / nf
    twiddle = np.concatenate([np.cos(angle), -np.sin(angle)], 0)
    phase = 2.0 * np.pi * (np.outer(n, n) % LANES) / LANES
    c, s = np.cos(phase), np.sin(phase)
    scale = 1.0 / math.sqrt(nf * nt)
    table = np.block([[c, -s], [s, c]]) * scale
    high = table.astype(np.float32).astype(jnp.bfloat16)
    low = (table - high.astype(np.float64)).astype(np.float32).astype(jnp.bfloat16)
    return (
        taper.reshape(radix, LANES).astype(np.float32),
        twiddle.astype(np.float32),
        high,
        low,
    )


def turn(value, k, size):
    re, im = value
    if k == 0:
        return value
    if 4 * k == size:
        return im, -re
    if 8 * k == size:
        h = math.sqrt(0.5)
        return (re + im) * h, (im - re) * h
    if 8 * k == 3 * size:
        h = math.sqrt(0.5)
        return (im - re) * h, (re + im) * -h
    c, s = math.cos(2 * math.pi * k / size), math.sin(2 * math.pi * k / size)
    return re * c + im * s, im * c - re * s


def short_dft(values):
    size = len(values)
    if size == 1:
        return values
    even, odd = short_dft(values[0::2]), short_dft(values[1::2])
    odd = [turn(v, k, size) for k, v in enumerate(odd)]
    low = [(a + c, b + d) for (a, b), (c, d) in zip(even, odd)]
    high = [(a - c, b - d) for (a, b), (c, d) in zip(even, odd)]
    return low + high


def swap_groups(parts):
    n = len(parts)
    width = LANES // n
    lane = lax.broadcasted_iota(jnp.int32, parts[0].shape, 1)
    bit = 1
    while bit < n:
        upper = (lane // (width * bit)) % 2 == 1
        fresh = list(parts)
        for i in range(n):
            if i & bit:
                continue
            j = i | bit
            fresh[i] = jnp.where(upper, pltpu.roll(parts[j], width * bit, 1), parts[i])
            fresh[j] = jnp.where(upper, parts[j], pltpu.roll(parts[i], LANES - width * bit, 1))
        parts = fresh
        bit *= 2
    return parts


def kernel(
    n, vis, flags, taper, twiddle, high, low, cross, band,
    x, zhi, zlo, spec, send, recv, gram, back, home,
    in_sem, send_sem, recv_sem, own_sem, back_sem, home_sem, last_sem,
):
    _, count, nt, nf = vis.shape
    radix = nf // LANES
    bands = nf // BW // n
    total = n * count
    depth = recv.shape[1]
    piece = depth // CHUNKS
    steps = nt // CHUNKS
    half = nt // 2
    me = lax.axis_index("bl")
    order = sorted(range(1, n), key=lambda k: -min(k, n - k))

    def fetch(h, p, q):
        return pltpu.make_async_copy(
            vis.at[p, :, pl.ds(h * half, half), pl.ds(q * LANES, LANES)],
            x.at[p, q, :, pl.ds(h * half, half), :],
            in_sem.at[h, p, q],
        )

    places = [(p, q) for p in range(2) for q in range(radix)]
    for h in range(2):
        for p, q in places:
            fetch(h, p, q).start()

    barrier = pltpu.get_barrier_semaphore()
    for k in order:
        pl.semaphore_signal(
            barrier, inc=1, device_id={"bl": lax.rem(me + k, n)}, device_id_type=MESH
        )

    rows_view = x.reshape(2 * radix * count * nt, LANES)

    def forward(c, peer, slot):
        return pltpu.make_async_remote_copy(
            src_ref=send.at[peer, :, pl.ds(pl.multiple_of(c * piece, LANES), piece)],
            dst_ref=recv.at[
                pl.ds(pl.multiple_of(slot * count, count), count),
                pl.ds(pl.multiple_of(c * piece, LANES), piece),
            ],
            send_sem=send_sem.at[c, peer],
            recv_sem=recv_sem.at[c, slot],
            device_id={"bl": peer},
            device_id_type=MESH,
        )

    def own(c):
        columns = pl.ds(pl.multiple_of(c * piece, LANES), piece)
        return pltpu.make_async_copy(
            send.at[me, :, columns],
            recv.at[pl.ds(pl.multiple_of(me * count, count), count), columns],
            own_sem.at[c],
        )

    def produce(c):
        keep = flags[...].astype(F32)
        weights = [keep[:, q : q + 1] * taper[q : q + 1, :] for q in range(radix)]
        for s in range(steps):
            t = c * steps + s
            values = []
            for q in range(radix):
                pair = [
                    rows_view[pl.ds((p * radix + q) * count * nt + t, count, stride=nt), :]
                    * weights[q]
                    for p in range(2)
                ]
                values.append(tuple(pair))
            for r, (re, im) in enumerate(short_dft(values)):
                if r:
                    c_r, s_r = twiddle[r : r + 1, :], twiddle[radix + r : radix + r + 1, :]
                    re, im = re * c_r - im * s_r, re * s_r + im * c_r
                z = jnp.concatenate([re, im], 1)
                z_hi = z.astype(BF16)
                at = pl.ds((s * radix + r) * count, count)
                zhi[at, :] = z_hi
                zlo[at, :] = (z - z_hi.astype(F32)).astype(BF16)
        dot = functools.partial(jnp.dot, preferred_element_type=F32)
        spec[...] = (
            dot(zhi[...], high[...]) + dot(zlo[...], high[...]) + dot(zhi[...], low[...])
        )
        blocks = [
            spec[pl.ds((s * radix + r) * count, count), pl.ds(p * LANES, LANES)]
            for s in range(steps)
            for p in range(2)
            for r in range(radix)
        ]
        for g in range(len(blocks) // n):
            at = pl.ds(pl.multiple_of(c * piece + g * LANES, LANES), LANES)
            for d, block in enumerate(swap_groups(blocks[g * n : (g + 1) * n])):
                send[d, :, at] = block.astype(BF16)

    def ship(c):
        own(c).start()
        for k in order:
            forward(c, lax.rem(me + k, n), me).start()

    for h in range(2):
        for p, q in places:
            fetch(h, p, q).wait()
        if h == 0:
            produce(0)
            pl.semaphore_wait(barrier, n - 1)
            ship(0)
        first = max(1, h * CHUNKS // 2)

        @pl.loop(first, (h + 1) * CHUNKS // 2)
        def _(c):
            produce(c)
            ship(c)

    lane = lax.broadcasted_iota(jnp.int32, (1, piece), 1)
    group = lane % (LANES // n) // (BW // radix)
    masks = [(group == kb).astype(BF16) for kb in range(bands)]
    gram[...] = jnp.zeros_like(gram)

    @pl.loop(0, CHUNKS)
    def _(c):
        own(c).wait()
        for k in reversed(order):
            peer = lax.rem(me + k, n)
            forward(c, peer, peer).wait_recv()
        block = recv[:, pl.ds(pl.multiple_of(c * piece, LANES), piece)]
        for kb in range(bands):
            gram[kb] += lax.dot_general(
                block, block * masks[kb], (((1,), (1,)), ((), ())), preferred_element_type=F32
            )

    row = lax.broadcasted_iota(jnp.int32, (total, total), 0)
    col = lax.broadcasted_iota(jnp.int32, (total, total), 1)
    spot = lax.broadcasted_iota(jnp.int32, (count, total), 1)
    line = lax.broadcasted_iota(jnp.int32, (count, total), 0)
    extra = jnp.zeros((count, total), F32)
    for kb in range(bands):
        power = gram[kb]
        back[:, kb * count : (kb + 1) * count, :] = power.astype(BF16).reshape(n, count, total)
        side = jnp.sum(jnp.where(row != col, power, 0.0), axis=0, keepdims=True)
        side = jnp.sum(side, axis=1, keepdims=True) * (1.0 / total)
        extra += jnp.where(spot == me * bands + kb, side, 0.0)
    rest = extra - extra.astype(BF16).astype(F32)
    extra = jnp.where(line == 0, extra, jnp.where(line == 1, rest, 0.0)).astype(BF16)
    for d in range(n):
        back[d, bands * count :, :] = extra

    def homeward(peer, slot):
        return pltpu.make_async_remote_copy(
            src_ref=back.at[peer],
            dst_ref=home.at[slot],
            send_sem=back_sem.at[peer],
            recv_sem=home_sem.at[slot],
            device_id={"bl": peer},
            device_id_type=MESH,
        )

    stay = pltpu.make_async_copy(back.at[me], home.at[me], last_sem)
    stay.start()
    for k in order:
        homeward(lax.rem(me + k, n), me).start()

    @pl.loop(0, CHUNKS)
    def _(c):
        for k in order:
            peer = lax.rem(me + k, n)
            forward(c, peer, me).wait_send()

    stay.wait()
    for k in reversed(order):
        peer = lax.rem(me + k, n)
        homeward(peer, peer).wait_recv()
    sums = jnp.zeros((count, total), F32)
    for d in range(n):
        for kb in range(bands):
            cross[d * bands + kb] = home[d, kb * count : (kb + 1) * count, :].astype(F32)
        sums += home[d, bands * count :, :].astype(F32)
    band[...] = jnp.sum(sums, axis=0, keepdims=True)
    for k in order:
        homeward(lax.rem(me + k, n), me).wait_send()


def shards(n, visibilities, flags):
    _, count, nt, nf = visibilities.shape
    radix = nf // LANES
    total = n * count
    bands = nf // BW // n
    depth = nt * 2 * nf // n
    consts = [jnp.asarray(v) for v in tables(nf, nt)]
    rows = nt // CHUNKS * radix * count
    vmem = pl.BlockSpec(memory_space=pltpu.VMEM)
    dma = pltpu.SemaphoreType.DMA
    cross, band = pl.pallas_call(
        functools.partial(kernel, n),
        out_shape=[
            jax.ShapeDtypeStruct((nf // BW, count, total), F32),
            jax.ShapeDtypeStruct((1, total), F32),
        ],
        in_specs=[pl.BlockSpec(memory_space=pl.ANY)] + [vmem] * 5,
        out_specs=[vmem, vmem],
        scratch_shapes=[
            pltpu.VMEM((2, radix, count, nt, LANES), F32),
            pltpu.VMEM((rows, 2 * LANES), BF16),
            pltpu.VMEM((rows, 2 * LANES), BF16),
            pltpu.VMEM((rows, 2 * LANES), F32),
            pltpu.VMEM((n, count, depth), BF16),
            pltpu.VMEM((total, depth), BF16),
            pltpu.VMEM((bands, total, total), F32),
            pltpu.VMEM((n, (bands + 1) * count, total), BF16),
            pltpu.VMEM((n, (bands + 1) * count, total), BF16),
            dma((2, 2, radix)),
            dma((CHUNKS, n)),
            dma((CHUNKS, n)),
            dma((CHUNKS,)),
            dma((n,)),
            dma((n,)),
            dma,
        ],
        compiler_params=pltpu.CompilerParams(
            collective_id=0, has_side_effects=True, vmem_limit_bytes=56 * 1024 * 1024
        ),
    )(visibilities, flags, *consts)
    return cross, band[0, : nf // BW]


def solution(mesh):
    return jax.shard_map(
        functools.partial(shards, mesh.shape["bl"]),
        mesh=mesh,
        in_specs=(P(None, ("group", "bl"), None, None), P(("group", "bl"), None)),
        out_specs=(P(None, ("group", "bl"), None), P("group")),
        check_vma=False,
    )
```

time: 278 us -> 43.8 us (0.16)
  waiting for transfers between devices: 124 us -> 0 us
  matrix products: 85.7 us -> 0 us
  Pallas kernels: 0 us -> 38.7 us
  local copies, waits for them, and re-layouts: 24.7 us -> 4.15 us
  blocking collectives: 18.5 us -> 0 us
  between operations: 14.1 us -> 0.64 us
  other arithmetic: 10.5 us -> 0 us
    all_gather x1 -> x0, waiting for transfers between devices: 124 us -> none  [shards(): whole = lax.all_gather(own, 'bl', axis=1, tiled=True)]
    dot_general x5 -> x0, matrix products: 85.7 us -> none  [the longest x1 20 us: delay_spectra(): jnp.dot(imag_rows, cosine, precision=high)]
    pallas_call x0 -> x1, Pallas kernels: none -> 38.7 us  [shards(): pl.pallas_call(functools.partial(kernel, n), out_shape=[jax.ShapeDtypeStr...]
    convert_element_type x3 -> x0, local copies, waits for them, and re-layouts: 20.2 us -> none  [the longest x2 20.2 us: delay_spectra(): return stacked.reshape(NF // BW, count, NT * 2 * BW).astype(jnp.bfloat16)]
    psum x1 -> x0, blocking collectives: 18.5 us -> none  [shards(): bandpower = lax.psum(partial_sum, 'bl') / total]
    convert_element_type x2 -> x0, other arithmetic: 5.19 us -> none  [the longest x1 4.5 us: delay_spectra(): return stacked.reshape(NF // BW, count, NT * 2 * BW).astype(jnp.bfloat16)]
    another operation x2 -> x0, local copies, waits for them, and re-layouts: 4.14 us -> none  [delay_spectra(): jnp.stack([real_out.reshape(count, NT, NF), imag_out.reshape(count, NT, N...]
    unnamed x2, local copies, waits for them, and re-layouts: 0.01 us -> 3.02 us
  transfers between devices with their start and end apart: 1 -> 0, of which waited for: 1 -> 0; matrix products, arithmetic and copies ran while one was open for 1% -> 0% of each run, Pallas kernels for 0% -> 0%
where the time goes in v1:
time: 43.8 us; the launch traced here: 43.5 us
  Pallas kernels  38.7 us (88%)
  local copies, waits for them, and re-layouts  4.15 us (9%)
  between operations  0.64 us (1%)
    pallas_call x1, Pallas kernels, shards(): pl.pallas_call(functools.partial(kernel, n), out_shape=[jax.ShapeDtypeStr...  38.7 us
    unnamed x2, local copies, waits for them, and re-layouts  3.02 us
    squeeze x1, local copies, waits for them, and re-layouts, shards(): return (cross, band[0, :nf // BW])  1.13 us

profile of v1, /device:TPU:0, one launch (start us, length us, event | category | flops | bytes accessed | tf_op | source)
XLA Modules:
  0.0 43.5 jit_solution(7436140396041034176)
XLA Ops:
  0.6 1.4 %copy.8.flags = s32[16,8]{1,0:T(8,128)} copy(s32[16,8]{0,1:T(8,128)} %param.7) | data formatting | bytes 1024 | tf_op args[1]
  2.0 38.7 %shard_map.77 = (f32[32,16,128]{2,1,0:T(8,128)}, f32[1,128]{1,0:T(1,128)}) custom-call(f32[2,16,16,1024]{3,2,1,0:T(8,128)} %vis.1, s32[16,8]{1,0:T(8,128)} %copy.8.flags, f32[8,128]{1,0:T(8,128)} %constant.8.clone.taper, f32[16,128]{1,0:T(8,128)} %constant.9.clone.twiddle, bf16[256,256]{1,0:T(8,128)(2,1)} %constant.10.clone.high, ...), custom_call_target="tpu_custom_call" | custom-call | tf_op jit(solution)/shard_map/pallas_call | solution.py:278
  40.7 1.1 %slice_bitcast_fusion = f32[32]{0:T(128)} fusion(f32[1,128]{1,0:T(1,128)} %get-tuple-element.5), kind=kLoop, calls=%fused_computation | loop fusion | bytes 256 | tf_op jit(solution)/shard_map/squeeze | solution.py:308
  41.8 1.7 %copy.10 = f32[32,16,128]{2,1,0:T(8,128)} copy(f32[32,16,128]{2,1,0:T(8,128)} %get-tuple-element.8) | data formatting | bytes 524288

commit v2 on v1

--- a/solution.py
+++ b/solution.py
@@ -85,9 +85,9 @@
 
 
 def kernel(
-    n, vis, flags, taper, twiddle, high, low, cross, band,
-    x, zhi, zlo, spec, send, recv, gram, back, home,
-    in_sem, send_sem, recv_sem, own_sem, back_sem, home_sem, last_sem,
+    n, vis, flags_hbm, curves_hbm, table_hbm, home,
+    x, flags, curves, table, weight, zhi, zlo, spec, send, recv, gram, back,
+    in_sem, small_sem, send_sem, recv_sem, own_sem, back_sem, home_sem, last_sem,
 ):
     _, count, nt, nf = vis.shape
     radix = nf // LANES
@@ -100,6 +100,12 @@
     me = lax.axis_index("bl")
     order = sorted(range(1, n), key=lambda k: -min(k, n - k))
 
+    barrier = pltpu.get_barrier_semaphore()
+    for k in order:
+        pl.semaphore_signal(
+            barrier, inc=1, device_id={"bl": lax.rem(me + k, n)}, device_id_type=MESH
+        )
+
     def fetch(h, p, q):
         return pltpu.make_async_copy(
             vis.at[p, :, pl.ds(h * half, half), pl.ds(q * LANES, LANES)],
@@ -107,16 +113,27 @@
             in_sem.at[h, p, q],
         )
 
+    small = [
+        pltpu.make_async_copy(source, target, small_sem.at[i])
+        for i, (source, target) in enumerate(
+            [(flags_hbm, flags), (curves_hbm, curves), (table_hbm, table)]
+        )
+    ]
     places = [(p, q) for p in range(2) for q in range(radix)]
+    for copy in small:
+        copy.start()
     for h in range(2):
         for p, q in places:
             fetch(h, p, q).start()
 
-    barrier = pltpu.get_barrier_semaphore()
-    for k in order:
-        pl.semaphore_signal(
-            barrier, inc=1, device_id={"bl": lax.rem(me + k, n)}, device_id_type=MESH
-        )
+    for copy in small:
+        copy.wait()
+    diagonal = lax.broadcasted_iota(jnp.int32, (count, count), 0) == lax.broadcasted_iota(
+        jnp.int32, (count, count), 1
+    )
+    for q in range(radix):
+        keep = jnp.where(diagonal, flags[q : q + 1, :].astype(F32), 0.0)
+        weight[q] = jnp.sum(keep, axis=1, keepdims=True) * curves[q : q + 1, :]
 
     rows_view = x.reshape(2 * radix * count * nt, LANES)
 
@@ -142,21 +159,20 @@
         )
 
     def produce(c):
-        keep = flags[...].astype(F32)
-        weights = [keep[:, q : q + 1] * taper[q : q + 1, :] for q in range(radix)]
         for s in range(steps):
             t = c * steps + s
             values = []
             for q in range(radix):
                 pair = [
                     rows_view[pl.ds((p * radix + q) * count * nt + t, count, stride=nt), :]
-                    * weights[q]
+                    * weight[q]
                     for p in range(2)
                 ]
                 values.append(tuple(pair))
             for r, (re, im) in enumerate(short_dft(values)):
                 if r:
-                    c_r, s_r = twiddle[r : r + 1, :], twiddle[radix + r : radix + r + 1, :]
+                    c_r = curves[radix + r : radix + r + 1, :]
+                    s_r = curves[2 * radix + r : 2 * radix + r + 1, :]
                     re, im = re * c_r - im * s_r, re * s_r + im * c_r
                 z = jnp.concatenate([re, im], 1)
                 z_hi = z.astype(BF16)
@@ -165,7 +181,7 @@
                 zlo[at, :] = (z - z_hi.astype(F32)).astype(BF16)
         dot = functools.partial(jnp.dot, preferred_element_type=F32)
         spec[...] = (
-            dot(zhi[...], high[...]) + dot(zlo[...], high[...]) + dot(zhi[...], low[...])
+            dot(zhi[...], table[0]) + dot(zlo[...], table[0]) + dot(zhi[...], table[1])
         )
         blocks = [
             spec[pl.ds((s * radix + r) * count, count), pl.ds(p * LANES, LANES)]
@@ -255,14 +271,19 @@
     for k in reversed(order):
         peer = lax.rem(me + k, n)
         homeward(peer, peer).wait_recv()
+    for k in order:
+        homeward(lax.rem(me + k, n), me).wait_send()
+
+
+def unpack(bands, home, cross, band):
+    n, _, total = home.shape
+    count = cross.shape[1]
     sums = jnp.zeros((count, total), F32)
     for d in range(n):
         for kb in range(bands):
             cross[d * bands + kb] = home[d, kb * count : (kb + 1) * count, :].astype(F32)
         sums += home[d, bands * count :, :].astype(F32)
-    band[...] = jnp.sum(sums, axis=0, keepdims=True)
-    for k in order:
-        homeward(lax.rem(me + k, n), me).wait_send()
+    band[...] = jnp.sum(sums, axis=0, keepdims=True)[:, : n * bands]
 
 
 def shards(n, visibilities, flags):
@@ -271,20 +292,25 @@
     total = n * count
     bands = nf // BW // n
     depth = nt * 2 * nf // n
-    consts = [jnp.asarray(v) for v in tables(nf, nt)]
+    taper, twiddle, high, low = tables(nf, nt)
+    curves = jnp.asarray(np.concatenate([taper, twiddle], 0))
+    table = jnp.asarray(np.stack([high, low]))
+    turned = flags.T
     rows = nt // CHUNKS * radix * count
     vmem = pl.BlockSpec(memory_space=pltpu.VMEM)
+    anywhere = pl.BlockSpec(memory_space=pl.ANY)
     dma = pltpu.SemaphoreType.DMA
-    cross, band = pl.pallas_call(
+    home = pl.pallas_call(
         functools.partial(kernel, n),
-        out_shape=[
-            jax.ShapeDtypeStruct((nf // BW, count, total), F32),
-            jax.ShapeDtypeStruct((1, total), F32),
-        ],
-        in_specs=[pl.BlockSpec(memory_space=pl.ANY)] + [vmem] * 5,
-        out_specs=[vmem, vmem],
+        out_shape=jax.ShapeDtypeStruct((n, (bands + 1) * count, total), BF16),
+        in_specs=[pl.BlockSpec(memory_space=pltpu.HBM)] * 4,
+        out_specs=anywhere,
         scratch_shapes=[
             pltpu.VMEM((2, radix, count, nt, LANES), F32),
+            pltpu.VMEM(turned.shape, turned.dtype),
+            pltpu.VMEM(curves.shape, curves.dtype),
+            pltpu.VMEM(table.shape, table.dtype),
+            pltpu.VMEM((radix, count, LANES), F32),
             pltpu.VMEM((rows, 2 * LANES), BF16),
             pltpu.VMEM((rows, 2 * LANES), BF16),
             pltpu.VMEM((rows, 2 * LANES), F32),
@@ -292,8 +318,8 @@
             pltpu.VMEM((total, depth), BF16),
             pltpu.VMEM((bands, total, total), F32),
             pltpu.VMEM((n, (bands + 1) * count, total), BF16),
-            pltpu.VMEM((n, (bands + 1) * count, total), BF16),
             dma((2, 2, radix)),
+            dma((3,)),
             dma((CHUNKS, n)),
             dma((CHUNKS, n)),
             dma((CHUNKS,)),
@@ -302,10 +328,20 @@
             dma,
         ],
         compiler_params=pltpu.CompilerParams(
-            collective_id=0, has_side_effects=True, vmem_limit_bytes=56 * 1024 * 1024
+            collective_id=0, has_side_effects=True, vmem_limit_bytes=24 * 1024 * 1024
         ),
-    )(visibilities, flags, *consts)
-    return cross, band[0, : nf // BW]
+    )(visibilities, turned, curves, table)
+    cross, band = pl.pallas_call(
+        functools.partial(unpack, bands),
+        out_shape=[
+            jax.ShapeDtypeStruct((nf // BW, count, total), F32),
+            jax.ShapeDtypeStruct((1, nf // BW), F32),
+        ],
+        in_specs=[vmem],
+        out_specs=[vmem, vmem],
+        compiler_params=pltpu.CompilerParams(vmem_limit_bytes=8 * 1024 * 1024),
+    )(home)
+    return cross, band.reshape(nf // BW)
 
 
 def solution(mesh):

time: 43.8 us -> 42.5 us (0.970)
  Pallas kernels: 38.7 us -> 37.7 us
    squeeze x1 -> x0, local copies, waits for them, and re-layouts: 1.13 us -> none  [shards(): return (cross, band[0, :nf // BW])]
    pallas_call x1 -> x2, Pallas kernels: 38.7 us -> 37.7 us  [the longest x1 36.9 us: shards(): pl.pallas_call(functools.partial(kernel, n), out_shape=jax.ShapeDtypeStru...]
    unnamed x2 -> x8, local copies, waits for them, and re-layouts: 3.02 us -> 3.93 us
where the time goes in v2:
time: 42.5 us; the launch traced here: 42.2 us
  Pallas kernels  37.7 us (89%)
  local copies, waits for them, and re-layouts  3.93 us (9%)
  between operations  0.65 us (2%)
    pallas_call x1, Pallas kernels, shards(): pl.pallas_call(functools.partial(kernel, n), out_shape=jax.ShapeDtypeStru...  36.9 us
    unnamed x8, local copies, waits for them, and re-layouts  3.93 us

profile of v2, /device:TPU:0, one launch (start us, length us, event | category | flops | bytes accessed | tf_op | source)
XLA Modules:
  0.0 42.2 jit_solution(930867761795250982)
XLA Ops:
  0.6 0.0 copy-start
  0.6 1.6 %copy-done = f32[2,16,16,1024]{3,2,1,0:T(8,128)S(1)} copy-done((f32[2,16,16,1024]{3,2,1,0:T(8,128)S(1)}, f32[2,16,16,1024]{3,2,1,0:T(8,128)}, u32[]{:S(2)}) %copy-start) | copy-done | bytes 2097176
  2.2 0.0 copy-start.1
  2.2 0.9 %copy-done.1 = bf16[2,256,256]{2,1,0:T(8,128)(2,1)S(1)} copy-done((bf16[2,256,256]{2,1,0:T(8,128)(2,1)S(1)}, bf16[2,256,256]{2,1,0:T(8,128)(2,1)}, u32[]{:S(2)}) %copy-start.1) | copy-done | bytes 262168
  3.2 0.0 copy-start.2
  3.2 0.7 %copy-done.2 = f32[24,128]{1,0:T(8,128)S(1)} copy-done((f32[24,128]{1,0:T(8,128)S(1)}, f32[24,128]{1,0:T(8,128)}, u32[]{:S(2)}) %copy-start.2) | copy-done | bytes 12312
  3.9 0.0 copy-start.3
  3.9 0.7 %copy-done.3 = s32[16,8]{0,1:T(8,128)S(1)} copy-done((s32[16,8]{0,1:T(8,128)S(1)}, s32[16,8]{0,1:T(8,128)}, u32[]{:S(2)}) %copy-start.3) | copy-done | bytes 536
  4.6 36.9 %shard_map.59.home = bf16[8,80,128]{2,1,0:T(8,128)(2,1)S(1)} custom-call(f32[2,16,16,1024]{3,2,1,0:T(8,128)S(1)} %copy-done, s32[8,16]{1,0:T(8,128)S(1)} %bitcast.2, f32[24,128]{1,0:T(8,128)S(1)} %copy-done.2, bf16[2,256,256]{2,1,0:T(8,128)(2,1)S(1)} %copy-done.1), custom_call_target="tpu_custom_call" | custom-call | tf_op jit(solution)/shard_map/pallas_call | solution.py:303
  41.5 0.7 %shard_map.60 = (f32[32,16,128]{2,1,0:T(8,128)}, f32[1,32]{1,0:T(1,128)}) custom-call(bf16[8,80,128]{2,1,0:T(8,128)(2,1)S(1)} %shard_map.59.home), custom_call_target="tpu_custom_call" | custom-call | tf_op jit(solution)/shard_map/pallas_call | solution.py:334
Async XLA Ops:
  0.6 1.6 %copy-start = (f32[2,16,16,1024]{3,2,1,0:T(8,128)S(1)}, f32[2,16,16,1024]{3,2,1,0:T(8,128)}, u32[]{:S(2)}) copy-start(f32[2,16,16,1024]{3,2,1,0:T(8,128)} %vis.1) | copy-start | bytes 6291460
  2.2 0.9 %copy-start.1 = (bf16[2,256,256]{2,1,0:T(8,128)(2,1)S(1)}, bf16[2,256,256]{2,1,0:T(8,128)(2,1)}, u32[]{:S(2)}) copy-start(bf16[2,256,256]{2,1,0:T(8,128)(2,1)} %constant.5.clone.table_hbm) | copy-start | bytes 786436
  3.2 0.7 %copy-start.2 = (f32[24,128]{1,0:T(8,128)S(1)}, f32[24,128]{1,0:T(8,128)}, u32[]{:S(2)}) copy-start(f32[24,128]{1,0:T(8,128)} %constant.4.clone.curves_hbm) | copy-start | bytes 36868
  3.9 0.7 %copy-start.3 = (s32[16,8]{0,1:T(8,128)S(1)}, s32[16,8]{0,1:T(8,128)}, u32[]{:S(2)}) copy-start(s32[16,8]{0,1:T(8,128)} %param.5) | copy-start | bytes 1540

commit v3 on v2

--- a/solution.py
+++ b/solution.py
@@ -328,7 +328,7 @@
             dma,
         ],
         compiler_params=pltpu.CompilerParams(
-            collective_id=0, has_side_effects=True, vmem_limit_bytes=24 * 1024 * 1024
+            collective_id=0, has_side_effects=True, vmem_limit_bytes=56 * 1024 * 1024
         ),
     )(visibilities, turned, curves, table)
     cross, band = pl.pallas_call(

time: 42.5 us -> 39.5 us (0.929)
  local copies, waits for them, and re-layouts: 3.93 us -> 0.91 us
    unnamed x8 -> x2, local copies, waits for them, and re-layouts: 3.93 us -> 0.91 us
where the time goes in v3:
time: 39.5 us; the launch traced here: 39.3 us
  Pallas kernels  37.8 us (96%)
  local copies, waits for them, and re-layouts  0.91 us (2%)
  between operations  0.65 us (2%)
    pallas_call x1, Pallas kernels, shards(): pl.pallas_call(functools.partial(kernel, n), out_shape=jax.ShapeDtypeStru...  37.1 us
    unnamed x2, local copies, waits for them, and re-layouts  0.91 us

profile of v3, /device:TPU:0, one launch (start us, length us, event | category | flops | bytes accessed | tf_op | source)
XLA Modules:
  0.0 39.3 jit_solution(3763869458237383980)
XLA Ops:
  0.6 37.1 %shard_map.59.home = bf16[8,80,128]{2,1,0:T(8,128)(2,1)} custom-call(f32[2,16,16,1024]{3,2,1,0:T(8,128)} %vis.1, s32[8,16]{1,0:T(8,128)} %bitcast.2, f32[24,128]{1,0:T(8,128)} %constant.4.clone.curves_hbm, bf16[2,256,256]{2,1,0:T(8,128)(2,1)} %constant.5.clone.table_hbm), custom_call_target="tpu_custom_call" | custom-call | tf_op jit(solution)/shard_map/pallas_call | solution.py:303
  37.7 0.0 copy-start
  37.7 0.9 %copy-done = bf16[8,80,128]{2,1,0:T(8,128)(2,1)S(1)} copy-done((bf16[8,80,128]{2,1,0:T(8,128)(2,1)S(1)}, bf16[8,80,128]{2,1,0:T(8,128)(2,1)}, u32[]{:S(2)}) %copy-start) | copy-done | bytes 163864
  38.6 0.7 %shard_map.60 = (f32[32,16,128]{2,1,0:T(8,128)}, f32[1,32]{1,0:T(1,128)}) custom-call(bf16[8,80,128]{2,1,0:T(8,128)(2,1)S(1)} %copy-done), custom_call_target="tpu_custom_call" | custom-call | tf_op jit(solution)/shard_map/pallas_call | solution.py:334
Async XLA Ops:
  37.7 0.9 %copy-start = (bf16[8,80,128]{2,1,0:T(8,128)(2,1)S(1)}, bf16[8,80,128]{2,1,0:T(8,128)(2,1)}, u32[]{:S(2)}) copy-start(bf16[8,80,128]{2,1,0:T(8,128)(2,1)} %shard_map.59.home) | copy-start | bytes 491524
